TPU v7x, 32 devices: a whole 2x2x4 slice. The times are simulated.
32 devices in a mesh: dp: 8 (over y, x, core), tensor: 4 (over z).
Axes of the slice: x: 2, y: 2, z: 4, core: 2. Of those that a mesh axis runs over, the one named last changes fastest.
Arguments:
- tokens: bfloat16 [9216, 2048], P(('dp', 'tensor')), may hold values from -6 to 6
- segment_ids: int32 [8, 1152], P('dp'), may hold values from 0 to 2, as said below
- attn_gain: bfloat16 [1, 2048], P(None, 'dp'), may hold values from 0.5 to 1.5
- q_weight: bfloat16 [1, 2048, 2048], P(None, 'dp', 'tensor'), may hold values from -0.125 to 0.125
- key_matrix: bfloat16 [1, 2048, 1024], P(None, 'dp', 'tensor'), may hold values from -0.125 to 0.125
- value_matrix: bfloat16 [1, 2048, 1024], P(None, 'dp', 'tensor'), may hold values from -0.125 to 0.125
- o_weight: bfloat16 [1, 2048, 2048], P(None, 'dp', 'tensor'), may hold values from -0.75 to 0.75
- q_gain: bfloat16 [1, 128], P(None, 'dp'), may hold values from 0.25 to 1.75
- k_gain: bfloat16 [1, 128], P(None, 'dp'), may hold values from 0.25 to 1.75
- mlp_gain: bfloat16 [1, 2048], P(None, 'dp'), may hold values from 0.5 to 1.5
- gate_weight: bfloat16 [1, 2048, 6144], P(None, 'dp', 'tensor'), may hold values from -0.125 to 0.125
- up_weight: bfloat16 [1, 2048, 6144], P(None, 'dp', 'tensor'), may hold values from -0.125 to 0.125
- down_weight: bfloat16 [1, 2048, 6144], P(None, 'dp', 'tensor'), may hold values from -0.078125 to 0.078125
- cotangent: bfloat16 [9216, 2048], P(('dp', 'tensor')), may hold values from -6 to 6
Outputs:
- activations: bfloat16 [9216, 2048], P(('dp', 'tensor'))
- input_grad: float32 [9216, 2048], P(('dp', 'tensor'))
- attn_gain_grad: float32 [1, 2048], P(None, 'dp')
- q_weight_grad: float32 [1, 2048, 2048], P(None, 'dp', 'tensor')
- k_weight_grad: float32 [1, 2048, 1024], P(None, 'dp', 'tensor')
- v_weight_grad: float32 [1, 2048, 1024], P(None, 'dp', 'tensor')
- o_weight_grad: float32 [1, 2048, 2048], P(None, 'dp', 'tensor')
- q_gain_grad: float32 [1, 128], P(None, 'dp')
- k_gain_grad: float32 [1, 128], P(None, 'dp')
- mlp_gain_grad: float32 [1, 2048], P(None, 'dp')
- gate_weight_grad: float32 [1, 2048, 6144], P(None, 'dp', 'tensor')
- up_weight_grad: float32 [1, 2048, 6144], P(None, 'dp', 'tensor')
- down_weight_grad: float32 [1, 2048, 6144], P(None, 'dp', 'tensor')
Inputs may be any that keep to these rules, and one draw needn't show every extreme that they name: `segment_ids`: in each group the numbers never fall, each of the 3 sequences has one token or more, and one sequence of each group has exactly 1024 tokens.
All inputs are finite; a program needn't handle non-finite values.
Results may differ from a plain program's by a relative error of at most 0.02.
Values may be sent and summed in bfloat16 or wider, within the bound.
A program may use at most 192 MiB of HBM per device.

v0:
```python
import jax
import jax.numpy as jnp
from jax import lax
from jax.sharding import Mesh
from jax.sharding import PartitionSpec as P

HEAD_WIDTH = 128
DECODER_LAYERS = 1
NSEQ = 3
QBLOCK = 576
EPS = 1e-06
THETA = 1000000.0


def rms_scale(values, gain):
    return values * lax.rsqrt(jnp.mean(values * values, axis=-1, keepdims=True) + EPS) * gain


def rotate(values, cosine, sine_table):
    half_size = values.shape[-1] // 2
    turned = jnp.concatenate([-values[..., half_size:], values[..., :half_size]], axis=-1)
    return values * cosine + turned * sine_table


def swiglu(gate_raw, up_raw):
    return jax.nn.silu(gate_raw) * up_raw


def rotary_tables(sequence_labels, row_index):
    labels = jnp.arange(NSEQ, dtype=jnp.int32)
    starts = jnp.sum((sequence_labels[None, :] < labels[:, None]).astype(jnp.int32), axis=1)
    first_row = jnp.sum(
        jnp.where(sequence_labels[:, None] == labels[None, :], starts[None, :], 0), axis=1
    )
    position = (row_index - first_row).astype(jnp.float32)
    frequency = THETA ** (-(jnp.arange(HEAD_WIDTH // 2, dtype=jnp.float32) * (2.0 / HEAD_WIDTH)))
    angles = position[:, None] * frequency[None, :]
    cosine = jnp.concatenate([jnp.cos(angles), jnp.cos(angles)], axis=1)[:, None, :]
    sine_table = jnp.concatenate([jnp.sin(angles), jnp.sin(angles)], axis=1)[:, None, :]
    return (cosine, sine_table)


def contract_rows(left, right):
    return lax.dot_general(
        left, right, (((0,), (0,)), ((), ())), preferred_element_type=jnp.float32
    )


def contract_cols(left, right):
    return lax.dot_general(
        left, right, (((1,), (1,)), ((), ())), preferred_element_type=jnp.float32
    )


def block_items(queries, sequence_labels, columns):
    grouped_rows, kv_heads, repeat, head_size = queries.shape
    blocks = grouped_rows // QBLOCK
    return (
        (
            queries.reshape(blocks, QBLOCK, kv_heads, repeat, head_size),
            sequence_labels.reshape(blocks, QBLOCK),
            columns.reshape(blocks, QBLOCK),
        ),
        columns,
    )


def attend_forward(queries, key_reduced, value_reduced, sequence_labels, row_index):
    grouped_rows, kv_heads, repeat, head_size = queries.shape
    score_scale = HEAD_WIDTH ** (-0.5)
    items, columns = block_items(queries, sequence_labels, row_index)

    def one_block(block_item):
        q_block, id_block, row_block = block_item
        allowed = (id_block[:, None] == sequence_labels[None, :]) & (
            columns[None, :] <= row_block[:, None]
        )
        scores = (
            jnp.einsum("qgrd,kgd->grqk", q_block, key_reduced, preferred_element_type=jnp.float32)
            * score_scale
        )
        weights = jnp.where(allowed[None, None], jnp.exp(scores), 0.0)
        totals = jnp.sum(weights, axis=-1, keepdims=True)
        shares = (weights / totals).astype(jnp.bfloat16)
        attention_result = jnp.einsum(
            "grqk,kgd->qgrd", shares, value_reduced, preferred_element_type=jnp.float32
        )
        return (attention_result.astype(jnp.bfloat16), totals)

    attention_result, totals = lax.map(one_block, items)
    return (attention_result.reshape(grouped_rows, kv_heads * repeat * head_size), totals)


def attend_backward(
    queries, key_reduced, value_reduced, sequence_labels, row_index, totals, out_grad
):
    grouped_rows, kv_heads, repeat, head_size = queries.shape
    score_scale = HEAD_WIDTH ** (-0.5)
    items, columns = block_items(queries, sequence_labels, row_index)
    grad_blocks = out_grad.reshape(grouped_rows // QBLOCK, QBLOCK, kv_heads, repeat, head_size)

    def one_block(running, block_item):
        key_grad, value_grad = running
        q_block, id_block, row_block, total_block, grad_block = block_item
        allowed = (id_block[:, None] == sequence_labels[None, :]) & (
            columns[None, :] <= row_block[:, None]
        )
        scores = (
            jnp.einsum("qgrd,kgd->grqk", q_block, key_reduced, preferred_element_type=jnp.float32)
            * score_scale
        )
        shares = jnp.where(allowed[None, None], jnp.exp(scores), 0.0) / total_block
        low_shares = shares.astype(jnp.bfloat16)
        share_grad = jnp.einsum(
            "qgrd,kgd->grqk", grad_block, value_reduced, preferred_element_type=jnp.float32
        )
        row_inner = jnp.sum(shares * share_grad, axis=-1, keepdims=True)
        score_grad = (shares * (share_grad - row_inner)).astype(jnp.bfloat16)
        query_grad = (
            jnp.einsum(
                "grqk,kgd->qgrd", score_grad, key_reduced, preferred_element_type=jnp.float32
            )
            * score_scale
        )
        key_grad = (
            key_grad
            + jnp.einsum("grqk,qgrd->kgd", score_grad, q_block, preferred_element_type=jnp.float32)
            * score_scale
        )
        value_grad = value_grad + jnp.einsum(
            "grqk,qgrd->kgd", low_shares, grad_block, preferred_element_type=jnp.float32
        )
        return ((key_grad, value_grad), query_grad)

    zero_keys = jnp.zeros(key_reduced.shape, jnp.float32)
    (key_grad, value_grad), query_grad = lax.scan(
        one_block, (zero_keys, zero_keys), items + (totals, grad_blocks)
    )
    return (query_grad.reshape(grouped_rows, kv_heads * repeat, head_size), key_grad, value_grad)


def shift_perm(size, step):
    return [((place + step) % size, place) for place in range(size)]


def trade(values):
    return lax.ppermute(values, ("c", "h"), [(0, 0), (1, 2), (2, 1), (3, 3)])


def gather_tokens(own):
    places = lax.axis_size("l")
    parts = [own] + [lax.ppermute(own, "l", shift_perm(places, step)) for step in range(1, places)]
    half = jnp.concatenate(parts, axis=0)
    return jnp.concatenate([half, lax.ppermute(half, "c", shift_perm(2, 1))], axis=0)


def scatter_tokens(partial):
    places = lax.axis_size("l")
    half = partial.shape[0] // 2
    rows = half // places
    other = lax.ppermute(partial[half:].astype(jnp.bfloat16), "c", shift_perm(2, 1))
    total = partial[:half] + other.astype(jnp.float32)
    own = total[:rows]
    for step in range(1, places):
        sent = total[step * rows : (step + 1) * rows].astype(jnp.bfloat16)
        own = own + lax.ppermute(sent, "l", shift_perm(places, -step)).astype(jnp.float32)
    return own


def gather_weights(shard):
    core, upper = (lax.axis_index("c"), lax.axis_index("h"))
    far = lax.ppermute(shard, "h", shift_perm(2, 1))
    same = core == upper
    mine = jnp.where(same, shard, far)
    other = lax.ppermute(jnp.where(same, far, shard), "c", shift_perm(2, 1))
    rows = jnp.concatenate(
        [jnp.where(core == 0, mine, other), jnp.where(core == 0, other, mine)], axis=0
    )
    return lax.all_gather(rows, "d", axis=0, tiled=True)


def scatter_weights(partial):
    core, upper = (lax.axis_index("c"), lax.axis_index("h"))
    rows = lax.psum_scatter(partial.astype(jnp.bfloat16), "d", scatter_dimension=0, tiled=True)
    half = rows.shape[0] // 2
    first, second = (rows[:half], rows[half:])
    mine = jnp.where(core == 0, first, second)
    other = lax.ppermute(jnp.where(core == 0, second, first), "c", shift_perm(2, 1))
    same = core == upper
    far = lax.ppermute(jnp.where(same, other, mine), "h", shift_perm(2, 1))
    return jnp.where(same, mine, other).astype(jnp.float32) + far.astype(jnp.float32)


def per_device(
    tokens,
    segment_ids,
    attn_gain,
    q_weight,
    key_matrix,
    value_matrix,
    o_weight,
    q_gain,
    k_gain,
    mlp_gain,
    gate_weight,
    up_weight,
    down_weight,
    cotangent,
):
    width = attn_gain.shape[1] * lax.axis_size("d") * 2
    own_rows = tokens.shape[0]
    places = lax.axis_size("l")
    core, place = (lax.axis_index("c"), lax.axis_index("l"))
    q_cols, kv_cols, ff_cols = (q_weight.shape[2], key_matrix.shape[2], gate_weight.shape[2])
    tokens = trade(tokens)
    labels = trade(segment_ids)[0]
    attn_weights = gather_weights(
        jnp.concatenate([q_weight[0], key_matrix[0], value_matrix[0], o_weight[0]], axis=1)
    )
    mid_weights = gather_weights(jnp.concatenate([gate_weight[0], up_weight[0]], axis=1))
    down_full = gather_weights(down_weight[0])
    cotangent = trade(cotangent)
    gains = lax.all_gather(
        jnp.concatenate([attn_gain[0], mlp_gain[0], q_gain[0], k_gain[0]]), ("d", "c"), axis=0
    ).astype(jnp.float32)
    cut = attn_gain.shape[1]
    head_cut = q_gain.shape[1]
    attn_scale = gains[:, :cut].reshape(-1)
    mlp_scale = gains[:, cut : 2 * cut].reshape(-1)
    q_scale = gains[:, 2 * cut : 2 * cut + head_cut].reshape(-1)
    k_scale = gains[:, 2 * cut + head_cut :].reshape(-1)
    order = jnp.stack(
        [
            (core + core_step) % 2 * places + (place + step) % places
            for core_step in range(2)
            for step in range(places)
        ]
    )
    row_index = (
        order[:, None] * own_rows + jnp.arange(own_rows, dtype=jnp.int32)[None, :]
    ).reshape(-1)
    labels = labels.reshape(2 * places, own_rows)[order].reshape(-1)
    cosine, sine_table = rotary_tables(labels, row_index)
    stream = tokens.astype(jnp.float32)
    normed = gather_tokens(rms_scale(stream, attn_scale).astype(jnp.bfloat16))
    rows = normed.shape[0]
    head_count, kv_heads = (q_cols // HEAD_WIDTH, kv_cols // HEAD_WIDTH)
    q_full = attn_weights[:, :q_cols]
    k_full = attn_weights[:, q_cols : q_cols + kv_cols]
    v_full = attn_weights[:, q_cols + kv_cols : q_cols + 2 * kv_cols]
    o_full = attn_weights[:, q_cols + 2 * kv_cols :]
    queries = jnp.dot(normed, q_full, preferred_element_type=jnp.float32).reshape(
        rows, head_count, HEAD_WIDTH
    )
    keys = jnp.dot(normed, k_full, preferred_element_type=jnp.float32).reshape(
        rows, kv_heads, HEAD_WIDTH
    )
    value_reduced = (
        jnp.dot(normed, v_full, preferred_element_type=jnp.float32)
        .reshape(rows, kv_heads, HEAD_WIDTH)
        .astype(jnp.bfloat16)
    )
    query_reduced = rotate(rms_scale(queries, q_scale), cosine, sine_table).astype(jnp.bfloat16)
    key_reduced = rotate(rms_scale(keys, k_scale), cosine, sine_table).astype(jnp.bfloat16)
    query_reduced = query_reduced.reshape(rows, kv_heads, head_count // kv_heads, HEAD_WIDTH)
    attended, totals = attend_forward(query_reduced, key_reduced, value_reduced, labels, row_index)
    middle = stream + scatter_tokens(contract_cols(attended, o_full))
    normed_mid = gather_tokens(rms_scale(middle, mlp_scale).astype(jnp.bfloat16))
    gate_full, up_full = (mid_weights[:, :ff_cols], mid_weights[:, ff_cols:])
    gate_raw = jnp.dot(normed_mid, gate_full, preferred_element_type=jnp.float32)
    up_raw = jnp.dot(normed_mid, up_full, preferred_element_type=jnp.float32)
    hidden = swiglu(gate_raw, up_raw).astype(jnp.bfloat16)
    branch = scatter_tokens(contract_cols(hidden, down_full))
    activations = trade((middle + branch).astype(jnp.bfloat16))
    grad_rows = gather_tokens(cotangent)
    gradient = cotangent.astype(jnp.float32)
    down_grad = scatter_weights(contract_rows(grad_rows, hidden))
    hidden_grad = jnp.dot(grad_rows, down_full, preferred_element_type=jnp.float32)
    _, pull_back = jax.vjp(swiglu, gate_raw, up_raw)
    gate_grad, up_grad = pull_back(hidden_grad)
    gate_low = gate_grad.astype(jnp.bfloat16)
    up_low = up_grad.astype(jnp.bfloat16)
    mid_grad = scatter_weights(
        jnp.concatenate(
            [
                contract_rows(normed_mid, gate_low).astype(jnp.bfloat16),
                contract_rows(normed_mid, up_low).astype(jnp.bfloat16),
            ],
            axis=1,
        )
    )
    normed_grad = scatter_tokens(
        contract_cols(gate_low, gate_full) + contract_cols(up_low, up_full)
    )
    _, pull_norm = jax.vjp(rms_scale, middle, mlp_scale)
    middle_grad, mlp_gain_grad = pull_norm(normed_grad)
    gradient = gradient + middle_grad
    grad_rows = gather_tokens(gradient.astype(jnp.bfloat16))
    out_grad = jnp.dot(grad_rows, o_full, preferred_element_type=jnp.float32).astype(jnp.bfloat16)
    o_wgrad = contract_rows(grad_rows, attended)
    query_grad, key_grad, value_grad = attend_backward(
        query_reduced,
        key_reduced,
        value_reduced,
        labels,
        row_index,
        totals,
        out_grad.reshape(query_reduced.shape),
    )

    def query_path(raw_values, scales):
        return rotate(rms_scale(raw_values, scales), cosine, sine_table)

    _, pull_query = jax.vjp(query_path, queries, q_scale)
    query_raw_grad, q_gain_grad = pull_query(query_grad)
    _, pull_key = jax.vjp(query_path, keys, k_scale)
    key_raw_grad, k_gain_grad = pull_key(key_grad)
    query_back = query_raw_grad.reshape(rows, -1).astype(jnp.bfloat16)
    key_back = key_raw_grad.reshape(rows, -1).astype(jnp.bfloat16)
    value_back = value_grad.reshape(rows, -1).astype(jnp.bfloat16)
    attn_grad = scatter_weights(
        jnp.concatenate(
            [
                contract_rows(normed, query_back).astype(jnp.bfloat16),
                contract_rows(normed, key_back).astype(jnp.bfloat16),
                contract_rows(normed, value_back).astype(jnp.bfloat16),
                o_wgrad.astype(jnp.bfloat16),
            ],
            axis=1,
        )
    )
    normed_grad = scatter_tokens(
        contract_cols(query_back, q_full)
        + contract_cols(key_back, k_full)
        + contract_cols(value_back, v_full)
    )
    _, pull_norm = jax.vjp(rms_scale, stream, attn_scale)
    stream_grad, attn_gain_grad = pull_norm(normed_grad)
    gradient = gradient + stream_grad
    moved = trade(gradient.astype(jnp.bfloat16))
    gradient = jnp.where(core == lax.axis_index("h"), gradient, moved.astype(jnp.float32))
    sums = lax.psum(
        jnp.concatenate([attn_gain_grad, mlp_gain_grad, q_gain_grad, k_gain_grad]),
        ("d", "c", "h", "l"),
    )
    row = lax.axis_index("d") * 2 + core

    def owned(start, whole, part):
        return lax.dynamic_slice(sums[start : start + whole], (row * part,), (part,))[None]

    return (
        activations,
        gradient,
        owned(0, width, cut),
        attn_grad[None, :, :q_cols],
        attn_grad[None, :, q_cols : q_cols + kv_cols],
        attn_grad[None, :, q_cols + kv_cols : q_cols + 2 * kv_cols],
        attn_grad[None, :, q_cols + 2 * kv_cols :],
        owned(2 * width, HEAD_WIDTH, head_cut),
        owned(2 * width + HEAD_WIDTH, HEAD_WIDTH, head_cut),
        owned(width, width, cut),
        mid_grad[None, :, :ff_cols],
        mid_grad[None, :, ff_cols:],
        down_grad[None],
    )


def solution(mesh):
    dp, tensor = (mesh.shape["dp"], mesh.shape["tensor"])
    cut = Mesh(mesh.devices.reshape(dp // 2, 2, 2, tensor // 2), ("d", "c", "h", "l"))
    rows, cols = (("d", "c"), ("h", "l"))
    tokens, labels = (P(rows + cols, None), P(rows, None))
    gain, weight = (P(None, rows), P(None, rows, cols))
    return jax.shard_map(
        per_device,
        mesh=cut,
        in_specs=(
            tokens,
            labels,
            gain,
            weight,
            weight,
            weight,
            weight,
            gain,
            gain,
            gain,
            weight,
            weight,
            weight,
            tokens,
        ),
        out_specs=(
            tokens,
            tokens,
            gain,
            weight,
            weight,
            weight,
            weight,
            gain,
            gain,
            gain,
            weight,
            weight,
            weight,
        ),
        check_vma=False,
    )
```

profile of v0, /device:TPU:0, one launch (start us, length us, event | category | flops | bytes accessed | tf_op | source)
XLA Modules:
  0.0 1063.8 jit_solution(16250169278718028177)
XLA Ops:
  11.5 4.1 collective-permute-start.4
  15.6 34.4 %collective-permute-done.4 = bf16[256,1536]{0,1:T(8,128)(2,1)S(1)} collective-permute-done((bf16[256,1536]{0,1:T(8,128)(2,1)S(1)}, bf16[256,1536]{0,1:T(8,128)(2,1)S(1)}, u32[]{:S(2)}, u32[]{:S(2)}) %collective-permute-start.4) | collective-permute-done | bytes 786464 | tf_op jit(solution)/shard_map/ppermute | solution.py:172
  64.4 25.7 %all-reduce.4 = bf16[4352]{0:T(1024)(128)(2,1)S(1)} all-reduce(bf16[4352]{0:T(1024)(128)(2,1)S(1)} %dynamic-update-slice), channel_id=2, replica_groups=mesh['d'=4,'c'=2,'h'=2,'l'=2] {'d','c'}, use_global_device_ids=true, to_apply=%add.4 | all-reduce | flops 4352 | bytes 17408
  102.3 51.4 %collective-permute-done.10 = bf16[256,3072]{0,1:T(8,128)(2,1)} collective-permute-done((bf16[256,3072]{0,1:T(8,128)(2,1)}, bf16[256,3072]{0,1:T(8,128)(2,1)}, u32[]{:S(2)}, u32[]{:S(2)}) %collective-permute-start.10) | collective-permute-done | bytes 1572896 | tf_op jit(solution)/shard_map/ppermute | solution.py:172
  155.6 9.9 collective-permute-done.2
  167.3 6.5 collective-permute-start.3
  186.1 7.4 multiply_reduce_fusion.5
  204.5 5.0 copy.192
  210.8 7.0 fusion.70
  219.4 4.4 convolution_convert_fusion.8
  225.2 25.8 %while.28 = (s32[]{:T(128)}, bf16[2,576,2,2,128]{4,3,2,1,0:T(2,128)(2,1)S(1)}, f32[2,2,2,576,1]{3,2,1,4,0:T(2,128)}, s32[2,576]{1,0:T(2,128)}, s32[4,288]{1,0:T(...) while((s32[]{:T(128)}, ...), condition=%wide.region_7.8_spmd.clone, body=%wide.region_5.7_spmd.clone.sunk | while | flops 1379818368 | bytes 26884800 | solution.py:90
  252.1 15.6 %reshape.558 = bf16[1152,512]{1,0:T(8,128)(2,1)S(1)} reshape(bf16[2,576,2,2,128]{4,3,2,1,0:T(2,128)(2,1)} %copy-done.46) | data formatting | bytes 2359296 | tf_op jit(solution)/shard_map/reshape | solution.py:91
  267.7 4.6 fusion.72
  279.7 36.7 %collective-permute-done.12 = bf16[256,1536]{0,1:T(8,128)(2,1)S(1)} collective-permute-done((bf16[256,1536]{0,1:T(8,128)(2,1)S(1)}, bf16[256,1536]{0,1:T(8,128)(2,1)S(1)}, u32[]{:S(2)}, u32[]{:S(2)}) %collective-permute-start.12) | collective-permute-done | bytes 786464 | tf_op jit(solution)/shard_map/ppermute | solution.py:172
  316.6 10.4 collective-permute-start.17
  335.1 37.7 %collective-permute-done.7 = bf16[288,2048]{1,0:T(8,128)(2,1)} collective-permute-done((bf16[288,2048]{1,0:T(8,128)(2,1)}, bf16[288,2048]{1,0:T(8,128)(2,1)}, u32[]{:S(2)}, u32[]{:S(2)}) %collective-permute-start.7) | collective-permute-done | bytes 1179680 | tf_op jit(solution)/shard_map/ppermute | solution.py:166
  375.8 22.1 %collective-permute-done.18 = bf16[288,2048]{1,0:T(8,128)(2,1)S(1)} collective-permute-done((bf16[288,2048]{1,0:T(8,128)(2,1)}, bf16[288,2048]{1,0:T(8,128)(2,1)S(1)}, u32[]{:S(2)}, u32[]{:S(2)}) %collective-permute-start.18) | collective-permute-done | bytes 1179680 | tf_op jit(solution)/shard_map/ppermute | solution.py:152
  399.5 15.3 %collective-permute-done.8 = bf16[288,2048]{1,0:T(8,128)(2,1)S(1)} collective-permute-done((bf16[288,2048]{1,0:T(8,128)(2,1)S(1)}, bf16[288,2048]{1,0:T(8,128)(2,1)S(1)}, u32[]{:S(2)}, u32[]{:S(2)}) %collective-permute-start.8) | collective-permute-done | bytes 1179680 | tf_op jit(solution)/shard_map/ppermute | solution.py:152
  419.8 12.7 %fusion.52 = f32[1152,1536]{1,0:T(8,128)} fusion(bf16[2048,3072]{0,1:T(8,128)(2,1)} %all-gather.7.cloned.1.call-done, bf16[576,2048]{1,0:T(8,128)(2,1)} %collective-permute-done.9, bf16[288,2048]{1,0:T(8,128)(2,1)} %copy-done.51, bf16[288,2048]{1,0:T(8,128)(2,1)S(1)} %multiply_convert_fusion.2), kind=kOutput, calls=%fused_computation.75 | convolution fusion | flops 7261913088 | bytes 18087936 | tf_op jit(solution)/shard_map/dot_general | solution.py:271
  432.6 11.0 %fusion.56 = f32[1152,1536]{1,0:T(8,128)} fusion(bf16[2048,3072]{0,1:T(8,128)(2,1)S(1)} %copy-done.94, bf16[576,2048]{1,0:T(8,128)(2,1)} %collective-permute-done.9, bf16[288,2048]{1,0:T(8,128)(2,1)S(1)} %copy-done.52, bf16[288,2048]{1,0:T(8,128)(2,1)S(1)} %multiply_convert_fusion.2), kind=kOutput, calls=%fused_computation.79 | convolution fusion | flops 7261913088 | bytes 18087936 | tf_op jit(solution)/shard_map/dot_general | solution.py:270
  443.5 18.9 %multiply_convert_fusion = (bf16[1152,1536]{1,0:T(8,128)(2,1)}, bf16[1152,1536]{1,0:T(8,128)(2,1)}, bf16[1152,1536]{1,0:T(8,128)(2,1)}) fusion(f32[1152,1536]{1,0:T(8,128)} %fusion.56, f32[1152,1536]{1,0:T(8,128)} %fusion.52, bf16[1152,2048]{1,0:T(8,128)(2,1)} %copy-done.64, bf16[2048,1536]{0,1:T(8,128)(2,1)} %all-gather.9.cloned.1.call-done), kind=kOutput, calls=%fused_computation.69 | convolution fusion | flops 7276068864 | bytes 35782656 | tf_op jit(solution)/shard_map/dot_general | solution.py:278
  462.5 11.2 %fusion.54 = f32[1152,2048]{1,0:T(8,128)S(1)} fusion(bf16[1152,1536]{1,0:T(8,128)(2,1)} %get-tuple-element.461, bf16[2048,3072]{0,1:T(8,128)(2,1)} %all-gather.7.cloned.1.call-done), kind=kOutput, calls=%fused_computation.77 | convolution fusion | flops 7247757312 | bytes 19267584 | tf_op jit(solution)/shard_map/dot_general | solution.py:50
  473.7 10.9 %convolution_add_fusion.2 = f32[1152,2048]{1,0:T(8,128)S(1)} fusion(f32[1152,2048]{1,0:T(8,128)S(1)} %fusion.54, bf16[1152,1536]{1,0:T(8,128)(2,1)} %get-tuple-element.460, bf16[2048,3072]{0,1:T(8,128)(2,1)} %all-gather.7.cloned.1.call-done), kind=kOutput, calls=%fused_computation.62 | convolution fusion | flops 7250116608 | bytes 28704768 | tf_op jit(solution)/shard_map/dot_general | solution.py:50
  489.3 10.0 fusion.102
  506.5 25.5 %collective-permute-done.21 = bf16[288,2048]{1,0:T(8,128)(2,1)S(1)} collective-permute-done((bf16[288,2048]{1,0:T(8,128)(2,1)S(1)}, bf16[288,2048]{1,0:T(8,128)(2,1)S(1)}, u32[]{:S(2)}, u32[]{:S(2)}) %collective-permute-start.21) | collective-permute-done | bytes 1179680 | tf_op jit(solution)/shard_map/ppermute | solution.py:166
  533.4 23.3 %collective-permute-done.15 = bf16[288,2048]{1,0:T(8,128)(2,1)S(1)} collective-permute-done((bf16[288,2048]{1,0:T(8,128)(2,1)S(1)}, bf16[288,2048]{1,0:T(8,128)(2,1)S(1)}, u32[]{:S(2)}, u32[]{:S(2)}) %collective-permute-start.15) | collective-permute-done | bytes 1179680 | tf_op jit(solution)/shard_map/ppermute | solution.py:166
  556.7 4.4 fusion.95
  561.4 27.1 %collective-permute-done.22 = bf16[288,2048]{1,0:T(8,128)(2,1)S(1)} collective-permute-done((bf16[288,2048]{1,0:T(8,128)(2,1)S(1)}, bf16[288,2048]{1,0:T(8,128)(2,1)S(1)}, u32[]{:S(2)}, u32[]{:S(2)}) %collective-permute-start.22) | collective-permute-done | bytes 1179680 | tf_op jit(solution)/shard_map/ppermute | solution.py:152
  591.2 13.1 %convolution_convert_fusion = bf16[2048,1536]{0,1:T(8,128)(2,1)} fusion(bf16[1152,2048]{1,0:T(8,128)(2,1)} %copy-done.64, bf16[1152,1536]{1,0:T(8,128)(2,1)} %get-tuple-element.462), kind=kOutput, calls=%fused_computation.63 | convolution fusion | flops 7250903040 | bytes 14548992 | tf_op jit(solution)/shard_map/dot_general | solution.py:44
  604.4 6.3 convolution_convert_fusion.5
  614.5 55.6 %while.29 = (s32[]{:T(128)}, f32[1152,2,128]{0,2,1:T(8,128)S(1)}, f32[1152,2,128]{0,2,1:T(8,128)S(1)}, f32[2,576,2,2,128]{4,1,0,3,2:T(8,128)}, bf16[2,576,2,2,12...) while((s32[]{:T(128)}, f32[1152,2,128]{0,2,1:T(8,128)S(1)}, ...), condition=%wide.region_12.13_spmd.clone, body=%wide.region_10.12_spmd.clone.sunk | while | flops 3425033216 | bytes 203141424 | solution.py:136
  635.1 4.2 fusion.150
  662.7 4.4 fusion.150
  688.2 4.7 convolution_convert_fusion.4
  693.4 5.0 convolution_convert_fusion.3
  698.5 12.4 %pad_maximum_fusion.1 = bf16[2048,1536]{0,1:T(8,128)(2,1)} fusion(bf16[2048,512]{0,1:T(8,128)(2,1)S(1)} %convolution_convert_fusion.4, bf16[2048,256]{0,1:T(8,128)(2,1)S(1)} %convolution_convert_fusion.6, bf16[2048,256]{0,1:T(8,128)(2,1)S(1)} %convolution_convert_fusion.7, bf16[2048,512]{0,1:T(8,128)(2,1)S(1)} %convolution_convert_fusion.3), kind=kLoop, calls=%fused_computation.73 | loop fusion | flops 25165824 | bytes 12582912 | tf_op jit(solution)/shard_map/concatenate | solution.py:322
  712.5 11.2 %convolution_convert_fusion.2 = bf16[2048,1536]{0,1:T(8,128)(2,1)S(1)} fusion(bf16[1152,1536]{1,0:T(8,128)(2,1)} %get-tuple-element.461, bf16[576,2048]{1,0:T(8,128)(2,1)} %collective-permute-done.9, bf16[288,2048]{1,0:T(8,128)(2,1)S(1)} %copy-done.53, bf16[288,2048]{1,0:T(8,128)(2,1)S(1)} %copy-done.31), kind=kOutput, calls=%fused_computation.65 | convolution fusion | flops 7265058816 | bytes 14548992 | tf_op jit(solution)/shard_map/dot_general | solution.py:44
  723.7 10.2 convolution_convert_fusion.1
  733.9 15.3 %pad_maximum_fusion = bf16[2048,3072]{0,1:T(8,128)(2,1)} fusion(bf16[2048,1536]{0,1:T(8,128)(2,1)S(1)} %convolution_convert_fusion.1, bf16[2048,1536]{0,1:T(8,128)(2,1)S(1)} %convolution_convert_fusion.2), kind=kLoop, calls=%fused_computation.58 | loop fusion | flops 25165824 | bytes 25165824 | tf_op jit(solution)/shard_map/concatenate | solution.py:284
  750.6 4.2 fusion.74
  770.4 39.9 %collective-permute-done.25 = bf16[288,2048]{1,0:T(8,128)(2,1)S(1)} collective-permute-done((bf16[288,2048]{1,0:T(8,128)(2,1)}, bf16[288,2048]{1,0:T(8,128)(2,1)S(1)}, u32[]{:S(2)}, u32[]{:S(2)}) %collective-permute-start.25) | collective-permute-done | bytes 1179680 | tf_op jit(solution)/shard_map/ppermute | solution.py:166
  814.0 39.3 %psum.7 = f32[4352]{0:T(1024)S(1)} all-reduce(f32[4352]{0:T(1024)S(1)} %pad_maximum_fusion.20), channel_id=1, replica_groups=mesh['d'=4,'c'=2,'h'=2,'l'=2] {'d','c','h','l'}, use_global_device_ids=true, to_apply=%region_20.21 | all-reduce | flops 4352 | bytes 34816 | tf_op jit(solution)/shard_map/psum | solution.py:342
  855.3 4.6 fusion.93
  859.8 10.6 collective-permute-start.26
  877.6 27.4 %reduce-scatter.6.cloned.1.call-done = bf16[512,3072]{0,1:T(8,128)(2,1)} async-done(((bf16[2048,3072]{0,1:T(8,128)(2,1)}), bf16[512,3072]{0,1:T(8,128)(2,1)}) %reduce-scatter.6.cloned.1.call-update) | async-done | bytes 3145744 | tf_op jit(solution)/shard_map/reduce_scatter | solution.py:184
  920.6 79.5 %collective-permute-done.32 = bf16[256,1536]{0,1:T(8,128)(2,1)S(1)} collective-permute-done((bf16[256,1536]{0,1:T(8,128)(2,1)S(1)}, bf16[256,1536]{0,1:T(8,128)(2,1)S(1)}, u32[]{:S(2)}, u32[]{:S(2)}) %collective-permute-start.32) | collective-permute-done | bytes 786464 | tf_op jit(solution)/shard_map/ppermute | solution.py:190
  1004.6 12.4 %collective-permute-done.28 = bf16[256,1536]{0,1:T(8,128)(2,1)} collective-permute-done((bf16[256,1536]{0,1:T(8,128)(2,1)}, bf16[256,1536]{0,1:T(8,128)(2,1)}, u32[]{:S(2)}, u32[]{:S(2)}) %collective-permute-start.28) | collective-permute-done | bytes 786464 | tf_op jit(solution)/shard_map/ppermute | solution.py:190
  1029.6 20.6 %collective-permute-done.30 = bf16[256,3072]{0,1:T(8,128)(2,1)} collective-permute-done((bf16[256,3072]{0,1:T(8,128)(2,1)}, bf16[256,3072]{0,1:T(8,128)(2,1)}, u32[]{:S(2)}, u32[]{:S(2)}) %collective-permute-start.30) | collective-permute-done | bytes 1572896 | tf_op jit(solution)/shard_map/ppermute | solution.py:190
  (474 shorter events, 268.0 us)
Async XLA Ops:
  7.2 172.5 %all-gather.5.cloned.1.call-start = ((), (), s32[]{:S(2)}) async-start(), calls=%async_computation.3 | async-start | bytes 7864320 | tf_op jit(solution)/shard_map/all_gather | solution.py:179
  11.5 38.5 %collective-permute-start.4 = (bf16[256,1536]{0,1:T(8,128)(2,1)S(1)}, bf16[256,1536]{0,1:T(8,128)(2,1)S(1)}, u32[]{:S(2)}, u32[]{:S(2)}) collective-permute-start(bf16[256,1536]{0,1:T(8,128)(2,1)S(1)} %pad_maximum_fusion.15), channel_id=1, source_target_pairs={{2,0},{0,2},{3,1},{1,3},{6,4},{4,6},{7,5},{5,7},{10,8},{8,10},{11,... | collective-permute-start | bytes 2359304 | tf_op jit(solution)/shard_map/ppermute | solution.py:172
  50.2 2.4 collective-permute-start.5
  54.2 365.6 %all-gather.7.cloned.1.call-start = ((), (), s32[]{:S(2)}) async-start(), calls=%async_computation.4 | async-start | bytes 15728640 | tf_op jit(solution)/shard_map/all_gather | solution.py:179
  54.3 42.5 %collective-permute-start = (bf16[288,2048]{1,0:T(8,128)(2,1)}, bf16[288,2048]{1,0:T(8,128)(2,1)S(1)}, u32[]{:S(2)}, u32[]{:S(2)}) collective-permute-start(bf16[288,2048]{1,0:T(8,128)(2,1)} %param.18), channel_id=1, source_target_pairs={{0,0},{2,4},{4,2},{6,6},{1,1},{3,5},{5,3},{7,7},{8,8},{10,12},{12,... | collective-permute-start | bytes 3538952 | tf_op jit(solution)/shard_map/ppermute | solution.py:147
  56.3 38.7 %collective-permute-start.1 = (s32[1,1152]{1,0:T(1,128)}, s32[1,1152]{1,0:T(1,128)S(1)}, u32[]{:S(2)}, u32[]{:S(2)}) collective-permute-start(s32[1,1152]{1,0:T(1,128)} %param.19), channel_id=1, source_target_pairs={{0,0},{2,4},{4,2},{6,6},{1,1},{3,5},{5,3},{7,7},{8,8},{10,12},{12,... | collective-permute-start | bytes 13832 | tf_op jit(solution)/shard_map/ppermute | solution.py:147
  59.5 94.2 %collective-permute-start.10 = (bf16[256,3072]{0,1:T(8,128)(2,1)}, bf16[256,3072]{0,1:T(8,128)(2,1)}, u32[]{:S(2)}, u32[]{:S(2)}) collective-permute-start(bf16[256,3072]{0,1:T(8,128)(2,1)} %pad_maximum_fusion.13), channel_id=1, source_target_pairs={{2,0},{0,2},{3,1},{1,3},{6,4},{4,6},{7,5},{5,7},{10,8},{8,10},{11,... | collective-permute-start | bytes 4718600 | tf_op jit(solution)/shard_map/ppermute | solution.py:172
  97.1 58.4 %copy-start.82 = (f32[288]{0:T(512)}, f32[288]{0:T(512)S(1)}, u32[]{:S(2)}) copy-start(f32[288]{0:T(512)S(1)} %fusion.65) | copy-start | bytes 3460
  97.1 58.4 %copy-start.80 = (f32[288]{0:T(512)}, f32[288]{0:T(512)S(1)}, u32[]{:S(2)}) copy-start(f32[288]{0:T(512)S(1)} %fusion.88) | copy-start | bytes 3460
  97.4 68.1 %copy-start.32 = (bf16[288,2048]{1,0:T(8,128)(2,1)}, bf16[288,2048]{1,0:T(8,128)(2,1)S(1)}, u32[]{:S(2)}) copy-start(bf16[288,2048]{1,0:T(8,128)(2,1)S(1)} %fusion.60) | copy-start | bytes 3538948
  97.4 68.0 %collective-permute-start.2 = (bf16[288,2048]{1,0:T(8,128)(2,1)S(1)}, bf16[288,2048]{1,0:T(8,128)(2,1)S(1)}, u32[]{:S(2)}, u32[]{:S(2)}) collective-permute-start(bf16[288,2048]{1,0:T(8,128)(2,1)S(1)} %fusion.60), channel_id=1, source_target_pairs={{1,0},{0,1},{3,2},{2,3},{5,4},{4,5},{7,6},{6,7},{9,8},{8,9},{11,10... | collective-permute-start | bytes 3538952 | tf_op jit(solution)/shard_map/ppermute | solution.py:152
  155.5 20.9 %collective-permute-start.11 = (bf16[256,3072]{0,1:T(8,128)(2,1)S(1)}, bf16[256,3072]{0,1:T(8,128)(2,1)S(1)}, u32[]{:S(2)}, u32[]{:S(2)}) collective-permute-start(bf16[256,3072]{0,1:T(8,128)(2,1)S(1)} %broadcast_select_fusion.1), channel_id=1, source_target_pairs={{4,0},{0,4},{5,1},{1,5},{6,2},{2,6},{7,3},{3,7},{12,8},{8,12},{13,... | collective-permute-start | bytes 4718600 | tf_op jit(solution)/shard_map/ppermute | solution.py:175
  167.3 12.3 %collective-permute-start.3 = (bf16[576,2048]{1,0:T(8,128)(2,1)}, bf16[576,2048]{1,0:T(8,128)(2,1)}, u32[]{:S(2)}, u32[]{:S(2)}) collective-permute-start(bf16[576,2048]{1,0:T(8,128)(2,1)} %pad_maximum_fusion.6), channel_id=1, source_target_pairs={{4,0},{0,4},{5,1},{1,5},{6,2},{2,6},{7,3},{3,7},{12,8},{8,12},{13,... | collective-permute-start | bytes 7077896 | tf_op jit(solution)/shard_map/ppermute | solution.py:154
  179.2 264.3 %all-gather.9.cloned.1.call-start = ((), (), s32[]{:S(2)}) async-start(), calls=%async_computation.5 | async-start | bytes 7864320 | tf_op jit(solution)/shard_map/all_gather | solution.py:179
  276.7 50.3 %collective-permute-start.6 = (bf16[576,2048]{1,0:T(8,128)(2,1)}, bf16[576,2048]{1,0:T(8,128)(2,1)S(1)}, u32[]{:S(2)}, u32[]{:S(2)}) collective-permute-start(bf16[576,2048]{1,0:T(8,128)(2,1)} %slice.347), channel_id=1, source_target_pairs={{4,0},{0,4},{5,1},{1,5},{6,2},{2,6},{7,3},{3,7},{12,8},{8,12},{13,... | collective-permute-start | bytes 7077896 | tf_op jit(solution)/shard_map/ppermute | solution.py:161
  279.7 36.7 %collective-permute-start.12 = (bf16[256,1536]{0,1:T(8,128)(2,1)S(1)}, bf16[256,1536]{0,1:T(8,128)(2,1)S(1)}, u32[]{:S(2)}, u32[]{:S(2)}) collective-permute-start(bf16[256,1536]{0,1:T(8,128)(2,1)S(1)} %bitcast.247), channel_id=1, source_target_pairs={{2,0},{0,2},{3,1},{1,3},{6,4},{4,6},{7,5},{5,7},{10,8},{8,10},{11,... | collective-permute-start | bytes 2359304 | tf_op jit(solution)/shard_map/ppermute | solution.py:172
  316.5 14.9 %collective-permute-start.13 = (bf16[256,1536]{0,1:T(8,128)(2,1)S(1)}, bf16[256,1536]{0,1:T(8,128)(2,1)S(1)}, u32[]{:S(2)}, u32[]{:S(2)}) collective-permute-start(bf16[256,1536]{0,1:T(8,128)(2,1)S(1)} %broadcast_select_fusion.9), channel_id=1, source_target_pairs={{4,0},{0,4},{5,1},{1,5},{6,2},{2,6},{7,3},{3,7},{12,8},{8,12},{13,... | collective-permute-start | bytes 2359304 | tf_op jit(solution)/shard_map/ppermute | solution.py:175
  316.6 17.3 %collective-permute-start.17 = (bf16[288,2048]{1,0:T(8,128)(2,1)}, bf16[288,2048]{1,0:T(8,128)(2,1)}, u32[]{:S(2)}, u32[]{:S(2)}) collective-permute-start(bf16[288,2048]{1,0:T(8,128)(2,1)} %param.31), channel_id=1, source_target_pairs={{0,0},{2,4},{4,2},{6,6},{1,1},{3,5},{5,3},{7,7},{8,8},{10,12},{12,... | collective-permute-start | bytes 3538952 | tf_op jit(solution)/shard_map/ppermute | solution.py:147
  331.4 41.4 %collective-permute-start.7 = (bf16[288,2048]{1,0:T(8,128)(2,1)}, bf16[288,2048]{1,0:T(8,128)(2,1)}, u32[]{:S(2)}, u32[]{:S(2)}) collective-permute-start(bf16[288,2048]{1,0:T(8,128)(2,1)} %slice.351), channel_id=1, source_target_pairs={{1,0},{0,1},{3,2},{2,3},{5,4},{4,5},{7,6},{6,7},{9,8},{8,9},{11,10... | collective-permute-start | bytes 3538952 | tf_op jit(solution)/shard_map/ppermute | solution.py:166
  333.8 538.5 %reduce-scatter.8.cloned.1.call-start = ((), (), s32[]{:S(2)}) async-start(), calls=%async_computation.8 | async-start | bytes 7864320 | tf_op jit(solution)/shard_map/reduce_scatter | solution.py:184
  333.9 64.0 %collective-permute-start.18 = (bf16[288,2048]{1,0:T(8,128)(2,1)}, bf16[288,2048]{1,0:T(8,128)(2,1)S(1)}, u32[]{:S(2)}, u32[]{:S(2)}) collective-permute-start(bf16[288,2048]{1,0:T(8,128)(2,1)} %collective-permute-done.17), channel_id=1, source_target_pairs={{1,0},{0,1},{3,2},{2,3},{5,4},{4,5},{7,6},{6,7},{9,8},{8,9},{11,10... | collective-permute-start | bytes 3538952 | tf_op jit(solution)/shard_map/ppermute | solution.py:152
  375.7 56.8 %copy-start.30 = (bf16[288,2048]{1,0:T(8,128)(2,1)}, bf16[288,2048]{1,0:T(8,128)(2,1)S(1)}, u32[]{:S(2)}) copy-start(bf16[288,2048]{1,0:T(8,128)(2,1)S(1)} %multiply_convert_fusion.2) | copy-start | bytes 3538948
  375.8 39.0 %collective-permute-start.8 = (bf16[288,2048]{1,0:T(8,128)(2,1)S(1)}, bf16[288,2048]{1,0:T(8,128)(2,1)S(1)}, u32[]{:S(2)}, u32[]{:S(2)}) collective-permute-start(bf16[288,2048]{1,0:T(8,128)(2,1)S(1)} %multiply_convert_fusion.2), channel_id=1, source_target_pairs={{1,0},{0,1},{3,2},{2,3},{5,4},{4,5},{7,6},{6,7},{9,8},{8,9},{11,10... | collective-permute-start | bytes 3538952 | tf_op jit(solution)/shard_map/ppermute | solution.py:152
  399.4 17.3 %collective-permute-start.19 = (bf16[576,2048]{1,0:T(8,128)(2,1)S(1)}, bf16[576,2048]{1,0:T(8,128)(2,1)S(1)}, u32[]{:S(2)}, u32[]{:S(2)}) collective-permute-start(bf16[576,2048]{1,0:T(8,128)(2,1)S(1)} %pad_maximum_fusion.8), channel_id=1, source_target_pairs={{4,0},{0,4},{5,1},{1,5},{6,2},{2,6},{7,3},{3,7},{12,8},{8,12},{13,... | collective-permute-start | bytes 7077896 | tf_op jit(solution)/shard_map/ppermute | solution.py:154
  415.1 4.7 collective-permute-start.9
  485.0 14.9 %collective-permute-start.20 = (bf16[576,2048]{1,0:T(8,128)(2,1)S(1)}, bf16[576,2048]{1,0:T(8,128)(2,1)S(1)}, u32[]{:S(2)}, u32[]{:S(2)}) collective-permute-start(bf16[576,2048]{1,0:T(8,128)(2,1)S(1)} %slice.345), channel_id=1, source_target_pairs={{4,0},{0,4},{5,1},{1,5},{6,2},{2,6},{7,3},{3,7},{12,8},{8,12},{13,... | collective-permute-start | bytes 7077896 | tf_op jit(solution)/shard_map/ppermute | solution.py:161
  499.6 4.6 collective-permute-start.14
  503.1 28.9 %collective-permute-start.21 = (bf16[288,2048]{1,0:T(8,128)(2,1)S(1)}, bf16[288,2048]{1,0:T(8,128)(2,1)S(1)}, u32[]{:S(2)}, u32[]{:S(2)}) collective-permute-start(bf16[288,2048]{1,0:T(8,128)(2,1)S(1)} %slice.349), channel_id=1, source_target_pairs={{1,0},{0,1},{3,2},{2,3},{5,4},{4,5},{7,6},{6,7},{9,8},{8,9},{11,10... | collective-permute-start | bytes 3538952 | tf_op jit(solution)/shard_map/ppermute | solution.py:166
  505.5 51.2 %collective-permute-start.15 = (bf16[288,2048]{1,0:T(8,128)(2,1)S(1)}, bf16[288,2048]{1,0:T(8,128)(2,1)S(1)}, u32[]{:S(2)}, u32[]{:S(2)}) collective-permute-start(bf16[288,2048]{1,0:T(8,128)(2,1)S(1)} %slice.350), channel_id=1, source_target_pairs={{1,0},{0,1},{3,2},{2,3},{5,4},{4,5},{7,6},{6,7},{9,8},{8,9},{11,10... | collective-permute-start | bytes 3538952 | tf_op jit(solution)/shard_map/ppermute | solution.py:166
  561.1 27.4 %collective-permute-start.22 = (bf16[288,2048]{1,0:T(8,128)(2,1)S(1)}, bf16[288,2048]{1,0:T(8,128)(2,1)S(1)}, u32[]{:S(2)}, u32[]{:S(2)}) collective-permute-start(bf16[288,2048]{1,0:T(8,128)(2,1)S(1)} %get-tuple-element.446), channel_id=1, source_target_pairs={{1,0},{0,1},{3,2},{2,3},{5,4},{4,5},{7,6},{6,7},{9,8},{8,9},{11,10... | collective-permute-start | bytes 3538952 | tf_op jit(solution)/shard_map/ppermute | solution.py:152
  591.2 13.2 %collective-permute-start.23 = (bf16[576,2048]{1,0:T(8,128)(2,1)}, bf16[576,2048]{1,0:T(8,128)(2,1)}, u32[]{:S(2)}, u32[]{:S(2)}) collective-permute-start(bf16[576,2048]{1,0:T(8,128)(2,1)} %pad_maximum_fusion.9), channel_id=1, source_target_pairs={{4,0},{0,4},{5,1},{1,5},{6,2},{2,6},{7,3},{3,7},{12,8},{8,12},{13,... | collective-permute-start | bytes 7077896 | tf_op jit(solution)/shard_map/ppermute | solution.py:154
  604.3 270.4 %reduce-scatter.4.cloned.1.call-start = ((), (), s32[]{:S(2)}) async-start(), calls=%async_computation.6 | async-start | bytes 7864320 | tf_op jit(solution)/shard_map/reduce_scatter | solution.py:184
  710.9 194.1 %reduce-scatter.6.cloned.1.call-start = ((), (), s32[]{:S(2)}) async-start(), calls=%async_computation.7 | async-start | bytes 15728640 | tf_op jit(solution)/shard_map/reduce_scatter | solution.py:184
  760.5 4.6 collective-permute-start.24
  760.8 9.6 collective-permute-start.16
  769.6 40.8 %collective-permute-start.25 = (bf16[288,2048]{1,0:T(8,128)(2,1)}, bf16[288,2048]{1,0:T(8,128)(2,1)S(1)}, u32[]{:S(2)}, u32[]{:S(2)}) collective-permute-start(bf16[288,2048]{1,0:T(8,128)(2,1)} %slice.348), channel_id=1, source_target_pairs={{1,0},{0,1},{3,2},{2,3},{5,4},{4,5},{7,6},{6,7},{9,8},{8,9},{11,10... | collective-permute-start | bytes 3538952 | tf_op jit(solution)/shard_map/ppermute | solution.py:166
  770.4 43.6 %copy-start.78 = (f32[2048]{0:T(1024)S(1)}, f32[2048]{0:T(1024)}, u32[]{:S(2)}) copy-start(f32[2048]{0:T(1024)} %get-tuple-element.388) | copy-start | bytes 24580
  770.4 43.6 %copy-start.88 = (f32[128]{0:T(128)S(1)}, f32[128]{0:T(128)}, u32[]{:S(2)}) copy-start(f32[128]{0:T(128)} %get-tuple-element.394) | copy-start | bytes 1540
  770.4 43.6 %copy-start.89 = (f32[128]{0:T(128)S(1)}, f32[128]{0:T(128)}, u32[]{:S(2)}) copy-start(f32[128]{0:T(128)} %get-tuple-element.392) | copy-start | bytes 1540
  770.4 84.2 %copy-start.83 = (f32[288]{0:T(512)S(1)}, f32[288]{0:T(512)}, u32[]{:S(2)}) copy-start(f32[288]{0:T(512)} %copy-done.82) | copy-start | bytes 3460
  859.8 47.3 %collective-permute-start.26 = (bf16[288,2048]{1,0:T(8,128)(2,1)}, bf16[288,2048]{1,0:T(8,128)(2,1)}, u32[]{:S(2)}, u32[]{:S(2)}) collective-permute-start(bf16[288,2048]{1,0:T(8,128)(2,1)} %get-tuple-element.442), channel_id=1, source_target_pairs={{0,0},{2,4},{4,2},{6,6},{1,1},{3,5},{5,3},{7,7},{8,8},{10,12},{12,... | collective-permute-start | bytes 3538952 | tf_op jit(solution)/shard_map/ppermute | solution.py:147
  874.7 35.5 %collective-permute-start.31 = (bf16[256,1536]{0,1:T(8,128)(2,1)}, bf16[256,1536]{0,1:T(8,128)(2,1)S(1)}, u32[]{:S(2)}, u32[]{:S(2)}) collective-permute-start(bf16[256,1536]{0,1:T(8,128)(2,1)} %broadcast_select_fusion.13), channel_id=1, source_target_pairs={{4,0},{0,4},{5,1},{1,5},{6,2},{2,6},{7,3},{3,7},{12,8},{8,12},{13,... | collective-permute-start | bytes 2359304 | tf_op jit(solution)/shard_map/ppermute | solution.py:188
  877.3 36.5 %collective-permute-start.27 = (bf16[256,1536]{0,1:T(8,128)(2,1)}, bf16[256,1536]{0,1:T(8,128)(2,1)}, u32[]{:S(2)}, u32[]{:S(2)}) collective-permute-start(bf16[256,1536]{0,1:T(8,128)(2,1)} %broadcast_select_fusion.15), channel_id=1, source_target_pairs={{4,0},{0,4},{5,1},{1,5},{6,2},{2,6},{7,3},{3,7},{12,8},{8,12},{13,... | collective-permute-start | bytes 2359304 | tf_op jit(solution)/shard_map/ppermute | solution.py:188
  907.0 8.9 collective-permute-start.29
  911.2 88.8 %collective-permute-start.32 = (bf16[256,1536]{0,1:T(8,128)(2,1)S(1)}, bf16[256,1536]{0,1:T(8,128)(2,1)S(1)}, u32[]{:S(2)}, u32[]{:S(2)}) collective-permute-start(bf16[256,1536]{0,1:T(8,128)(2,1)S(1)} %broadcast_select_fusion.7), channel_id=1, source_target_pairs={{2,0},{0,2},{3,1},{1,3},{6,4},{4,6},{7,5},{5,7},{10,8},{8,10},{11,... | collective-permute-start | bytes 2359304 | tf_op jit(solution)/shard_map/ppermute | solution.py:190
  916.0 84.1 %copy-start.40 = (bf16[256,1536]{0,1:T(8,128)(2,1)S(1)}, bf16[256,1536]{0,1:T(8,128)(2,1)}, u32[]{:S(2)}) copy-start(bf16[256,1536]{0,1:T(8,128)(2,1)} %copy-done.39) | copy-start | bytes 2359300
  916.0 101.0 %collective-permute-start.28 = (bf16[256,1536]{0,1:T(8,128)(2,1)}, bf16[256,1536]{0,1:T(8,128)(2,1)}, u32[]{:S(2)}, u32[]{:S(2)}) collective-permute-start(bf16[256,1536]{0,1:T(8,128)(2,1)} %broadcast_select_fusion.8), channel_id=1, source_target_pairs={{2,0},{0,2},{3,1},{1,3},{6,4},{4,6},{7,5},{5,7},{10,8},{8,10},{11,... | collective-permute-start | bytes 2359304 | tf_op jit(solution)/shard_map/ppermute | solution.py:190
  917.7 132.5 %collective-permute-start.30 = (bf16[256,3072]{0,1:T(8,128)(2,1)}, bf16[256,3072]{0,1:T(8,128)(2,1)}, u32[]{:S(2)}, u32[]{:S(2)}) collective-permute-start(bf16[256,3072]{0,1:T(8,128)(2,1)} %broadcast_select_fusion), channel_id=1, source_target_pairs={{2,0},{0,2},{3,1},{1,3},{6,4},{4,6},{7,5},{5,7},{10,8},{8,10},{11,... | collective-permute-start | bytes 4718600 | tf_op jit(solution)/shard_map/ppermute | solution.py:190
  (95 other events, 637.1 us)
Sparse Core Ops, SparseCore 0:
  54.3 71.2 all-gather.4
  179.3 123.1 all-gather.6
  333.9 68.6 all-gather.8
  604.4 68.4 reduce-scatter.7
  711.0 68.9 reduce-scatter.3
  783.0 121.9 reduce-scatter.5
where the time goes:
time: 1070 us; the launch traced here: 1060 us
  waiting for transfers between devices  470 us (44%)
  matrix products  204 us (19%)
  local copies, waits for them, and re-layouts  134 us (13%)
  other arithmetic  119 us (11%)
  blocking collectives  65 us (6%)
  starting transfers between devices  55.5 us (5%)
  between operations  16.4 us (2%)
    ppermute x4, waiting for transfers between devices, scatter_tokens(): lax.ppermute(sent, 'l', shift_perm(places, -step)).astype(jnp.float32)  126 us
    ppermute x3, waiting for transfers between devices, gather_weights(): far = lax.ppermute(shard, 'h', shift_perm(2, 1))  122 us
    ppermute x3, waiting for transfers between devices, scatter_weights(): far = lax.ppermute(jnp.where(same, other, mine), 'h', shift_perm(2, 1))  113 us
    ppermute x4, waiting for transfers between devices, gather_tokens(): lax.ppermute(own, 'l', shift_perm(places, step))  74.4 us
    unnamed x210, local copies, waits for them, and re-layouts  51.2 us
    dot_general x7, matrix products, contract_rows(): lax.dot_general(left, right, (((0,), (0,)), ((), ())), preferred_element_...  50.7 us
    dot_general x7, matrix products, contract_cols(): lax.dot_general(left, right, (((1,), (1,)), ((), ())), preferred_element_...  46.3 us
    psum x1, blocking collectives, per_device(): lax.psum(jnp.concatenate([attn_gain_grad, mlp_gain_grad, q_gain_grad, k_g...  39.3 us
  transfers between devices with their start and end apart: 39, of which 19 were waited for; matrix products, arithmetic and copies ran while one was open for 34% of the time, Pallas kernels for 0%

commit v1 on v0

--- a/solution.py
+++ b/solution.py
@@ -339,10 +339,8 @@
     gradient = gradient + stream_grad
     moved = trade(gradient.astype(jnp.bfloat16))
     gradient = jnp.where(core == lax.axis_index("h"), gradient, moved.astype(jnp.float32))
-    sums = lax.psum(
-        jnp.concatenate([attn_gain_grad, mlp_gain_grad, q_gain_grad, k_gain_grad]),
-        ("d", "c", "h", "l"),
-    )
+    m = jnp.concatenate([attn_gain_grad, mlp_gain_grad, q_gain_grad, k_gain_grad])
+    sums = lax.all_gather(m, ("d", "c", "h", "l")).sum(axis=0)
     row = lax.axis_index("d") * 2 + core
 
     def owned(start, whole, part):

time: 1070 us -> 1080 us (level)
  blocking collectives: 65 us -> 97.4 us
  waiting for transfers between devices: 470 us -> 441 us
    all_gather x0 -> x1, blocking collectives: none -> 71.7 us  [per_device(): sums = lax.all_gather(m, ('d', 'c', 'h', 'l')).sum(axis=0)]
    psum x1 -> x0, blocking collectives: 39.3 us -> none  [per_device(): lax.psum(jnp.concatenate([attn_gain_grad, mlp_gain_grad, q_gain_grad, k_g...]
    reduce_scatter x3, waiting for transfers between devices: 27.4 us -> 0.01 us  [scatter_weights(): lax.psum_scatter(partial.astype(jnp.bfloat16), 'd', scatter_dimension=0,...]
    unnamed x210 -> x211, local copies, waits for them, and re-layouts: 51.2 us -> 51.2 us
  transfers between devices with their start and end apart: 39 -> 39, of which waited for: 19 -> 18; matrix products, arithmetic and copies ran while one was open for 34% -> 33% of each run, Pallas kernels for 0% -> 0%
where the time goes in v1:
time: 1080 us; the launch traced here: 1070 us
  waiting for transfers between devices  441 us (41%)
  matrix products  204 us (19%)
  local copies, waits for them, and re-layouts  134 us (12%)
  other arithmetic  119 us (11%)
  blocking collectives  97.4 us (9%)
  starting transfers between devices  59.3 us (5%)
  between operations  16.5 us (2%)
    ppermute x4, waiting for transfers between devices, scatter_tokens(): lax.ppermute(sent, 'l', shift_perm(places, -step)).astype(jnp.float32)  126 us
    ppermute x3, waiting for transfers between devices, gather_weights(): far = lax.ppermute(shard, 'h', shift_perm(2, 1))  122 us
    ppermute x3, waiting for transfers between devices, scatter_weights(): far = lax.ppermute(jnp.where(same, other, mine), 'h', shift_perm(2, 1))  111 us
    ppermute x4, waiting for transfers between devices, gather_tokens(): lax.ppermute(own, 'l', shift_perm(places, step))  74.4 us
    all_gather x1, blocking collectives, per_device(): sums = lax.all_gather(m, ('d', 'c', 'h', 'l')).sum(axis=0)  71.7 us
    unnamed x211, local copies, waits for them, and re-layouts  51.2 us
    dot_general x7, matrix products, contract_rows(): lax.dot_general(left, right, (((0,), (0,)), ((), ())), preferred_element_...  50.7 us
    dot_general x7, matrix products, contract_cols(): lax.dot_general(left, right, (((1,), (1,)), ((), ())), preferred_element_...  46.3 us
  transfers between devices with their start and end apart: 39, of which 18 were waited for; matrix products, arithmetic and copies ran while one was open for 33% of the time, Pallas kernels for 0%

profile of v1, /device:TPU:0, one launch (start us, length us, event | category | flops | bytes accessed | tf_op | source)
XLA Modules:
  0.0 1071.7 jit_solution(17313919162058695017)
XLA Ops:
  11.5 4.1 collective-permute-start.4
  15.6 34.4 %collective-permute-done.4 = bf16[256,1536]{0,1:T(8,128)(2,1)S(1)} collective-permute-done((bf16[256,1536]{0,1:T(8,128)(2,1)S(1)}, bf16[256,1536]{0,1:T(8,128)(2,1)S(1)}, u32[]{:S(2)}, u32[]{:S(2)}) %collective-permute-start.4) | collective-permute-done | bytes 786464 | tf_op jit(solution)/shard_map/ppermute | solution.py:172
  64.4 25.7 %all-reduce.4 = bf16[4352]{0:T(1024)(128)(2,1)S(1)} all-reduce(bf16[4352]{0:T(1024)(128)(2,1)S(1)} %dynamic-update-slice), channel_id=2, replica_groups=mesh['d'=4,'c'=2,'h'=2,'l'=2] {'d','c'}, use_global_device_ids=true, to_apply=%add.4 | all-reduce | flops 4352 | bytes 17408
  102.3 51.4 %collective-permute-done.10 = bf16[256,3072]{0,1:T(8,128)(2,1)} collective-permute-done((bf16[256,3072]{0,1:T(8,128)(2,1)}, bf16[256,3072]{0,1:T(8,128)(2,1)}, u32[]{:S(2)}, u32[]{:S(2)}) %collective-permute-start.10) | collective-permute-done | bytes 1572896 | tf_op jit(solution)/shard_map/ppermute | solution.py:172
  155.6 9.9 collective-permute-done.2
  167.3 6.5 collective-permute-start.3
  186.1 7.4 multiply_reduce_fusion.5
  204.5 5.0 copy.228
  210.8 7.0 fusion.70
  219.4 4.4 convolution_convert_fusion.8
  225.2 25.8 %while.28 = (s32[]{:T(128)}, bf16[2,576,2,2,128]{4,3,2,1,0:T(2,128)(2,1)S(1)}, f32[2,2,2,576,1]{3,2,1,4,0:T(2,128)}, s32[2,576]{1,0:T(2,128)}, s32[4,288]{1,0:T(...) while((s32[]{:T(128)}, ...), condition=%wide.region_7.8_spmd.clone, body=%wide.region_5.7_spmd.clone.sunk | while | flops 1379818368 | bytes 26884800 | solution.py:90
  252.1 15.6 %reshape.558 = bf16[1152,512]{1,0:T(8,128)(2,1)S(1)} reshape(bf16[2,576,2,2,128]{4,3,2,1,0:T(2,128)(2,1)} %copy-done.46) | data formatting | bytes 2359296 | tf_op jit(solution)/shard_map/reshape | solution.py:91
  267.7 4.6 fusion.72
  279.7 36.7 %collective-permute-done.12 = bf16[256,1536]{0,1:T(8,128)(2,1)S(1)} collective-permute-done((bf16[256,1536]{0,1:T(8,128)(2,1)S(1)}, bf16[256,1536]{0,1:T(8,128)(2,1)S(1)}, u32[]{:S(2)}, u32[]{:S(2)}) %collective-permute-start.12) | collective-permute-done | bytes 786464 | tf_op jit(solution)/shard_map/ppermute | solution.py:172
  316.6 10.4 collective-permute-start.17
  335.1 37.7 %collective-permute-done.7 = bf16[288,2048]{1,0:T(8,128)(2,1)} collective-permute-done((bf16[288,2048]{1,0:T(8,128)(2,1)}, bf16[288,2048]{1,0:T(8,128)(2,1)}, u32[]{:S(2)}, u32[]{:S(2)}) %collective-permute-start.7) | collective-permute-done | bytes 1179680 | tf_op jit(solution)/shard_map/ppermute | solution.py:166
  375.8 22.1 %collective-permute-done.18 = bf16[288,2048]{1,0:T(8,128)(2,1)S(1)} collective-permute-done((bf16[288,2048]{1,0:T(8,128)(2,1)}, bf16[288,2048]{1,0:T(8,128)(2,1)S(1)}, u32[]{:S(2)}, u32[]{:S(2)}) %collective-permute-start.18) | collective-permute-done | bytes 1179680 | tf_op jit(solution)/shard_map/ppermute | solution.py:152
  399.5 15.3 %collective-permute-done.8 = bf16[288,2048]{1,0:T(8,128)(2,1)S(1)} collective-permute-done((bf16[288,2048]{1,0:T(8,128)(2,1)S(1)}, bf16[288,2048]{1,0:T(8,128)(2,1)S(1)}, u32[]{:S(2)}, u32[]{:S(2)}) %collective-permute-start.8) | collective-permute-done | bytes 1179680 | tf_op jit(solution)/shard_map/ppermute | solution.py:152
  419.8 12.7 %fusion.52 = f32[1152,1536]{1,0:T(8,128)} fusion(bf16[2048,3072]{0,1:T(8,128)(2,1)} %all-gather.9.cloned.1.call-done, bf16[576,2048]{1,0:T(8,128)(2,1)} %collective-permute-done.9, bf16[288,2048]{1,0:T(8,128)(2,1)} %copy-done.51, bf16[288,2048]{1,0:T(8,128)(2,1)S(1)} %multiply_convert_fusion.2), kind=kOutput, calls=%fused_computation.75 | convolution fusion | flops 7261913088 | bytes 18087936 | tf_op jit(solution)/shard_map/dot_general | solution.py:271
  432.6 11.0 %fusion.56 = f32[1152,1536]{1,0:T(8,128)} fusion(bf16[2048,3072]{0,1:T(8,128)(2,1)S(1)} %copy-done.94, bf16[576,2048]{1,0:T(8,128)(2,1)} %collective-permute-done.9, bf16[288,2048]{1,0:T(8,128)(2,1)S(1)} %copy-done.52, bf16[288,2048]{1,0:T(8,128)(2,1)S(1)} %multiply_convert_fusion.2), kind=kOutput, calls=%fused_computation.79 | convolution fusion | flops 7261913088 | bytes 18087936 | tf_op jit(solution)/shard_map/dot_general | solution.py:270
  443.5 18.9 %multiply_convert_fusion = (bf16[1152,1536]{1,0:T(8,128)(2,1)}, bf16[1152,1536]{1,0:T(8,128)(2,1)}, bf16[1152,1536]{1,0:T(8,128)(2,1)}) fusion(f32[1152,1536]{1,0:T(8,128)} %fusion.56, f32[1152,1536]{1,0:T(8,128)} %fusion.52, bf16[1152,2048]{1,0:T(8,128)(2,1)} %copy-done.64, bf16[2048,1536]{0,1:T(8,128)(2,1)} %all-gather.11.cloned.1.call-done), kind=kOutput, calls=%fused_computation.69 | convolution fusion | flops 7276068864 | bytes 35782656 | tf_op jit(solution)/shard_map/dot_general | solution.py:278
  462.5 11.2 %fusion.54 = f32[1152,2048]{1,0:T(8,128)S(1)} fusion(bf16[1152,1536]{1,0:T(8,128)(2,1)} %get-tuple-element.497, bf16[2048,3072]{0,1:T(8,128)(2,1)} %all-gather.9.cloned.1.call-done), kind=kOutput, calls=%fused_computation.77 | convolution fusion | flops 7247757312 | bytes 19267584 | tf_op jit(solution)/shard_map/dot_general | solution.py:50
  473.7 10.9 %convolution_add_fusion.2 = f32[1152,2048]{1,0:T(8,128)S(1)} fusion(f32[1152,2048]{1,0:T(8,128)S(1)} %fusion.54, bf16[1152,1536]{1,0:T(8,128)(2,1)} %get-tuple-element.496, bf16[2048,3072]{0,1:T(8,128)(2,1)} %all-gather.9.cloned.1.call-done), kind=kOutput, calls=%fused_computation.62 | convolution fusion | flops 7250116608 | bytes 28704768 | tf_op jit(solution)/shard_map/dot_general | solution.py:50
  489.3 10.0 fusion.102
  506.5 25.5 %collective-permute-done.21 = bf16[288,2048]{1,0:T(8,128)(2,1)S(1)} collective-permute-done((bf16[288,2048]{1,0:T(8,128)(2,1)S(1)}, bf16[288,2048]{1,0:T(8,128)(2,1)S(1)}, u32[]{:S(2)}, u32[]{:S(2)}) %collective-permute-start.21) | collective-permute-done | bytes 1179680 | tf_op jit(solution)/shard_map/ppermute | solution.py:166
  533.4 23.3 %collective-permute-done.15 = bf16[288,2048]{1,0:T(8,128)(2,1)S(1)} collective-permute-done((bf16[288,2048]{1,0:T(8,128)(2,1)S(1)}, bf16[288,2048]{1,0:T(8,128)(2,1)S(1)}, u32[]{:S(2)}, u32[]{:S(2)}) %collective-permute-start.15) | collective-permute-done | bytes 1179680 | tf_op jit(solution)/shard_map/ppermute | solution.py:166
  556.7 4.4 fusion.95
  561.4 27.1 %collective-permute-done.22 = bf16[288,2048]{1,0:T(8,128)(2,1)S(1)} collective-permute-done((bf16[288,2048]{1,0:T(8,128)(2,1)S(1)}, bf16[288,2048]{1,0:T(8,128)(2,1)S(1)}, u32[]{:S(2)}, u32[]{:S(2)}) %collective-permute-start.22) | collective-permute-done | bytes 1179680 | tf_op jit(solution)/shard_map/ppermute | solution.py:152
  591.2 13.1 %convolution_convert_fusion = bf16[2048,1536]{0,1:T(8,128)(2,1)} fusion(bf16[1152,2048]{1,0:T(8,128)(2,1)} %copy-done.64, bf16[1152,1536]{1,0:T(8,128)(2,1)} %get-tuple-element.498), kind=kOutput, calls=%fused_computation.63 | convolution fusion | flops 7250903040 | bytes 14548992 | tf_op jit(solution)/shard_map/dot_general | solution.py:44
  604.4 6.3 convolution_convert_fusion.5
  614.5 55.6 %while.29 = (s32[]{:T(128)}, f32[1152,2,128]{0,2,1:T(8,128)S(1)}, f32[1152,2,128]{0,2,1:T(8,128)S(1)}, f32[2,576,2,2,128]{4,1,0,3,2:T(8,128)}, bf16[2,576,2,2,12...) while((s32[]{:T(128)}, f32[1152,2,128]{0,2,1:T(8,128)S(1)}, ...), condition=%wide.region_12.13_spmd.clone, body=%wide.region_10.12_spmd.clone.sunk | while | flops 3425033216 | bytes 203141424 | solution.py:136
  635.1 4.2 fusion.150
  662.7 4.4 fusion.150
  688.2 4.7 convolution_convert_fusion.4
  693.4 5.0 convolution_convert_fusion.3
  698.5 12.4 %pad_maximum_fusion.1 = bf16[2048,1536]{0,1:T(8,128)(2,1)} fusion(bf16[2048,512]{0,1:T(8,128)(2,1)S(1)} %convolution_convert_fusion.4, bf16[2048,256]{0,1:T(8,128)(2,1)S(1)} %convolution_convert_fusion.6, bf16[2048,256]{0,1:T(8,128)(2,1)S(1)} %convolution_convert_fusion.7, bf16[2048,512]{0,1:T(8,128)(2,1)S(1)} %convolution_convert_fusion.3), kind=kLoop, calls=%fused_computation.73 | loop fusion | flops 25165824 | bytes 12582912 | tf_op jit(solution)/shard_map/concatenate | solution.py:322
  712.5 11.2 %convolution_convert_fusion.2 = bf16[2048,1536]{0,1:T(8,128)(2,1)S(1)} fusion(bf16[1152,1536]{1,0:T(8,128)(2,1)} %get-tuple-element.497, bf16[576,2048]{1,0:T(8,128)(2,1)} %collective-permute-done.9, bf16[288,2048]{1,0:T(8,128)(2,1)S(1)} %copy-done.53, bf16[288,2048]{1,0:T(8,128)(2,1)S(1)} %copy-done.31), kind=kOutput, calls=%fused_computation.65 | convolution fusion | flops 7265058816 | bytes 14548992 | tf_op jit(solution)/shard_map/dot_general | solution.py:44
  723.7 10.2 convolution_convert_fusion.1
  733.9 15.3 %pad_maximum_fusion = bf16[2048,3072]{0,1:T(8,128)(2,1)} fusion(bf16[2048,1536]{0,1:T(8,128)(2,1)S(1)} %convolution_convert_fusion.1, bf16[2048,1536]{0,1:T(8,128)(2,1)S(1)} %convolution_convert_fusion.2), kind=kLoop, calls=%fused_computation.58 | loop fusion | flops 25165824 | bytes 25165824 | tf_op jit(solution)/shard_map/concatenate | solution.py:284
  750.6 4.2 fusion.74
  770.4 39.9 %collective-permute-done.25 = bf16[288,2048]{1,0:T(8,128)(2,1)S(1)} collective-permute-done((bf16[288,2048]{1,0:T(8,128)(2,1)}, bf16[288,2048]{1,0:T(8,128)(2,1)S(1)}, u32[]{:S(2)}, u32[]{:S(2)}) %collective-permute-start.25) | collective-permute-done | bytes 1179680 | tf_op jit(solution)/shard_map/ppermute | solution.py:166
  814.0 71.7 %all-gather.2 = f32[32,1,4352]{2,1,0:T(1,128)S(1)} all-gather(f32[1,1,4352]{2,1,0:T(1,128)S(1)} %reshape.574), channel_id=3, replica_groups=mesh['d'=4,'c'=2,'h'=2,'l'=2] {'d','c','h','l'}, dimensions={0}, use_global_device_ids=true | all-gather | bytes 574464 | tf_op jit(solution)/shard_map/all_gather | solution.py:343
  888.0 5.0 fusion.93
  893.0 10.5 collective-permute-start.26
  917.0 6.2 collective-permute-start.32
  930.0 77.4 %collective-permute-done.32 = bf16[256,1536]{0,1:T(8,128)(2,1)S(1)} collective-permute-done((bf16[256,1536]{0,1:T(8,128)(2,1)S(1)}, bf16[256,1536]{0,1:T(8,128)(2,1)S(1)}, u32[]{:S(2)}, u32[]{:S(2)}) %collective-permute-start.32) | collective-permute-done | bytes 786464 | tf_op jit(solution)/shard_map/ppermute | solution.py:190
  1011.9 12.4 %collective-permute-done.28 = bf16[256,1536]{0,1:T(8,128)(2,1)} collective-permute-done((bf16[256,1536]{0,1:T(8,128)(2,1)}, bf16[256,1536]{0,1:T(8,128)(2,1)}, u32[]{:S(2)}, u32[]{:S(2)}) %collective-permute-start.28) | collective-permute-done | bytes 786464 | tf_op jit(solution)/shard_map/ppermute | solution.py:190
  1036.9 21.1 %collective-permute-done.30 = bf16[256,3072]{0,1:T(8,128)(2,1)} collective-permute-done((bf16[256,3072]{0,1:T(8,128)(2,1)}, bf16[256,3072]{0,1:T(8,128)(2,1)}, u32[]{:S(2)}, u32[]{:S(2)}) %collective-permute-start.30) | collective-permute-done | bytes 1572896 | tf_op jit(solution)/shard_map/ppermute | solution.py:190
  (476 shorter events, 265.9 us)
Async XLA Ops:
  7.2 172.5 %all-gather.7.cloned.1.call-start = ((), (), s32[]{:S(2)}) async-start(), calls=%async_computation.3 | async-start | bytes 7864320 | tf_op jit(solution)/shard_map/all_gather | solution.py:179
  11.5 38.5 %collective-permute-start.4 = (bf16[256,1536]{0,1:T(8,128)(2,1)S(1)}, bf16[256,1536]{0,1:T(8,128)(2,1)S(1)}, u32[]{:S(2)}, u32[]{:S(2)}) collective-permute-start(bf16[256,1536]{0,1:T(8,128)(2,1)S(1)} %pad_maximum_fusion.15), channel_id=1, source_target_pairs={{2,0},{0,2},{3,1},{1,3},{6,4},{4,6},{7,5},{5,7},{10,8},{8,10},{11,... | collective-permute-start | bytes 2359304 | tf_op jit(solution)/shard_map/ppermute | solution.py:172
  50.2 2.4 collective-permute-start.5
  54.2 365.6 %all-gather.9.cloned.1.call-start = ((), (), s32[]{:S(2)}) async-start(), calls=%async_computation.4 | async-start | bytes 15728640 | tf_op jit(solution)/shard_map/all_gather | solution.py:179
  54.3 42.5 %collective-permute-start = (bf16[288,2048]{1,0:T(8,128)(2,1)}, bf16[288,2048]{1,0:T(8,128)(2,1)S(1)}, u32[]{:S(2)}, u32[]{:S(2)}) collective-permute-start(bf16[288,2048]{1,0:T(8,128)(2,1)} %param.18), channel_id=1, source_target_pairs={{0,0},{2,4},{4,2},{6,6},{1,1},{3,5},{5,3},{7,7},{8,8},{10,12},{12,... | collective-permute-start | bytes 3538952 | tf_op jit(solution)/shard_map/ppermute | solution.py:147
  56.3 38.7 %collective-permute-start.1 = (s32[1,1152]{1,0:T(1,128)}, s32[1,1152]{1,0:T(1,128)S(1)}, u32[]{:S(2)}, u32[]{:S(2)}) collective-permute-start(s32[1,1152]{1,0:T(1,128)} %param.19), channel_id=1, source_target_pairs={{0,0},{2,4},{4,2},{6,6},{1,1},{3,5},{5,3},{7,7},{8,8},{10,12},{12,... | collective-permute-start | bytes 13832 | tf_op jit(solution)/shard_map/ppermute | solution.py:147
  59.5 94.2 %collective-permute-start.10 = (bf16[256,3072]{0,1:T(8,128)(2,1)}, bf16[256,3072]{0,1:T(8,128)(2,1)}, u32[]{:S(2)}, u32[]{:S(2)}) collective-permute-start(bf16[256,3072]{0,1:T(8,128)(2,1)} %pad_maximum_fusion.13), channel_id=1, source_target_pairs={{2,0},{0,2},{3,1},{1,3},{6,4},{4,6},{7,5},{5,7},{10,8},{8,10},{11,... | collective-permute-start | bytes 4718600 | tf_op jit(solution)/shard_map/ppermute | solution.py:172
  97.1 58.4 %copy-start.82 = (f32[288]{0:T(512)}, f32[288]{0:T(512)S(1)}, u32[]{:S(2)}) copy-start(f32[288]{0:T(512)S(1)} %fusion.65) | copy-start | bytes 3460
  97.1 58.4 %copy-start.80 = (f32[288]{0:T(512)}, f32[288]{0:T(512)S(1)}, u32[]{:S(2)}) copy-start(f32[288]{0:T(512)S(1)} %fusion.88) | copy-start | bytes 3460
  97.4 68.1 %copy-start.32 = (bf16[288,2048]{1,0:T(8,128)(2,1)}, bf16[288,2048]{1,0:T(8,128)(2,1)S(1)}, u32[]{:S(2)}) copy-start(bf16[288,2048]{1,0:T(8,128)(2,1)S(1)} %fusion.60) | copy-start | bytes 3538948
  97.4 68.0 %collective-permute-start.2 = (bf16[288,2048]{1,0:T(8,128)(2,1)S(1)}, bf16[288,2048]{1,0:T(8,128)(2,1)S(1)}, u32[]{:S(2)}, u32[]{:S(2)}) collective-permute-start(bf16[288,2048]{1,0:T(8,128)(2,1)S(1)} %fusion.60), channel_id=1, source_target_pairs={{1,0},{0,1},{3,2},{2,3},{5,4},{4,5},{7,6},{6,7},{9,8},{8,9},{11,10... | collective-permute-start | bytes 3538952 | tf_op jit(solution)/shard_map/ppermute | solution.py:152
  155.5 20.9 %collective-permute-start.11 = (bf16[256,3072]{0,1:T(8,128)(2,1)S(1)}, bf16[256,3072]{0,1:T(8,128)(2,1)S(1)}, u32[]{:S(2)}, u32[]{:S(2)}) collective-permute-start(bf16[256,3072]{0,1:T(8,128)(2,1)S(1)} %broadcast_select_fusion.1), channel_id=1, source_target_pairs={{4,0},{0,4},{5,1},{1,5},{6,2},{2,6},{7,3},{3,7},{12,8},{8,12},{13,... | collective-permute-start | bytes 4718600 | tf_op jit(solution)/shard_map/ppermute | solution.py:175
  167.3 12.3 %collective-permute-start.3 = (bf16[576,2048]{1,0:T(8,128)(2,1)}, bf16[576,2048]{1,0:T(8,128)(2,1)}, u32[]{:S(2)}, u32[]{:S(2)}) collective-permute-start(bf16[576,2048]{1,0:T(8,128)(2,1)} %pad_maximum_fusion.6), channel_id=1, source_target_pairs={{4,0},{0,4},{5,1},{1,5},{6,2},{2,6},{7,3},{3,7},{12,8},{8,12},{13,... | collective-permute-start | bytes 7077896 | tf_op jit(solution)/shard_map/ppermute | solution.py:154
  179.2 264.3 %all-gather.11.cloned.1.call-start = ((), (), s32[]{:S(2)}) async-start(), calls=%async_computation.5 | async-start | bytes 7864320 | tf_op jit(solution)/shard_map/all_gather | solution.py:179
  276.7 50.3 %collective-permute-start.6 = (bf16[576,2048]{1,0:T(8,128)(2,1)}, bf16[576,2048]{1,0:T(8,128)(2,1)S(1)}, u32[]{:S(2)}, u32[]{:S(2)}) collective-permute-start(bf16[576,2048]{1,0:T(8,128)(2,1)} %slice.347), channel_id=1, source_target_pairs={{4,0},{0,4},{5,1},{1,5},{6,2},{2,6},{7,3},{3,7},{12,8},{8,12},{13,... | collective-permute-start | bytes 7077896 | tf_op jit(solution)/shard_map/ppermute | solution.py:161
  279.7 36.7 %collective-permute-start.12 = (bf16[256,1536]{0,1:T(8,128)(2,1)S(1)}, bf16[256,1536]{0,1:T(8,128)(2,1)S(1)}, u32[]{:S(2)}, u32[]{:S(2)}) collective-permute-start(bf16[256,1536]{0,1:T(8,128)(2,1)S(1)} %bitcast.247), channel_id=1, source_target_pairs={{2,0},{0,2},{3,1},{1,3},{6,4},{4,6},{7,5},{5,7},{10,8},{8,10},{11,... | collective-permute-start | bytes 2359304 | tf_op jit(solution)/shard_map/ppermute | solution.py:172
  316.5 14.9 %collective-permute-start.13 = (bf16[256,1536]{0,1:T(8,128)(2,1)S(1)}, bf16[256,1536]{0,1:T(8,128)(2,1)S(1)}, u32[]{:S(2)}, u32[]{:S(2)}) collective-permute-start(bf16[256,1536]{0,1:T(8,128)(2,1)S(1)} %broadcast_select_fusion.9), channel_id=1, source_target_pairs={{4,0},{0,4},{5,1},{1,5},{6,2},{2,6},{7,3},{3,7},{12,8},{8,12},{13,... | collective-permute-start | bytes 2359304 | tf_op jit(solution)/shard_map/ppermute | solution.py:175
  316.6 17.3 %collective-permute-start.17 = (bf16[288,2048]{1,0:T(8,128)(2,1)}, bf16[288,2048]{1,0:T(8,128)(2,1)}, u32[]{:S(2)}, u32[]{:S(2)}) collective-permute-start(bf16[288,2048]{1,0:T(8,128)(2,1)} %param.31), channel_id=1, source_target_pairs={{0,0},{2,4},{4,2},{6,6},{1,1},{3,5},{5,3},{7,7},{8,8},{10,12},{12,... | collective-permute-start | bytes 3538952 | tf_op jit(solution)/shard_map/ppermute | solution.py:147
  331.4 41.4 %collective-permute-start.7 = (bf16[288,2048]{1,0:T(8,128)(2,1)}, bf16[288,2048]{1,0:T(8,128)(2,1)}, u32[]{:S(2)}, u32[]{:S(2)}) collective-permute-start(bf16[288,2048]{1,0:T(8,128)(2,1)} %slice.351), channel_id=1, source_target_pairs={{1,0},{0,1},{3,2},{2,3},{5,4},{4,5},{7,6},{6,7},{9,8},{8,9},{11,10... | collective-permute-start | bytes 3538952 | tf_op jit(solution)/shard_map/ppermute | solution.py:166
  333.8 571.7 %reduce-scatter.8.cloned.1.call-start = ((), (), s32[]{:S(2)}) async-start(), calls=%async_computation.8 | async-start | bytes 7864320 | tf_op jit(solution)/shard_map/reduce_scatter | solution.py:184
  333.9 64.0 %collective-permute-start.18 = (bf16[288,2048]{1,0:T(8,128)(2,1)}, bf16[288,2048]{1,0:T(8,128)(2,1)S(1)}, u32[]{:S(2)}, u32[]{:S(2)}) collective-permute-start(bf16[288,2048]{1,0:T(8,128)(2,1)} %collective-permute-done.17), channel_id=1, source_target_pairs={{1,0},{0,1},{3,2},{2,3},{5,4},{4,5},{7,6},{6,7},{9,8},{8,9},{11,10... | collective-permute-start | bytes 3538952 | tf_op jit(solution)/shard_map/ppermute | solution.py:152
  375.7 56.8 %copy-start.30 = (bf16[288,2048]{1,0:T(8,128)(2,1)}, bf16[288,2048]{1,0:T(8,128)(2,1)S(1)}, u32[]{:S(2)}) copy-start(bf16[288,2048]{1,0:T(8,128)(2,1)S(1)} %multiply_convert_fusion.2) | copy-start | bytes 3538948
  375.8 39.0 %collective-permute-start.8 = (bf16[288,2048]{1,0:T(8,128)(2,1)S(1)}, bf16[288,2048]{1,0:T(8,128)(2,1)S(1)}, u32[]{:S(2)}, u32[]{:S(2)}) collective-permute-start(bf16[288,2048]{1,0:T(8,128)(2,1)S(1)} %multiply_convert_fusion.2), channel_id=1, source_target_pairs={{1,0},{0,1},{3,2},{2,3},{5,4},{4,5},{7,6},{6,7},{9,8},{8,9},{11,10... | collective-permute-start | bytes 3538952 | tf_op jit(solution)/shard_map/ppermute | solution.py:152
  399.4 17.3 %collective-permute-start.19 = (bf16[576,2048]{1,0:T(8,128)(2,1)S(1)}, bf16[576,2048]{1,0:T(8,128)(2,1)S(1)}, u32[]{:S(2)}, u32[]{:S(2)}) collective-permute-start(bf16[576,2048]{1,0:T(8,128)(2,1)S(1)} %pad_maximum_fusion.8), channel_id=1, source_target_pairs={{4,0},{0,4},{5,1},{1,5},{6,2},{2,6},{7,3},{3,7},{12,8},{8,12},{13,... | collective-permute-start | bytes 7077896 | tf_op jit(solution)/shard_map/ppermute | solution.py:154
  415.1 4.7 collective-permute-start.9
  485.0 14.9 %collective-permute-start.20 = (bf16[576,2048]{1,0:T(8,128)(2,1)S(1)}, bf16[576,2048]{1,0:T(8,128)(2,1)S(1)}, u32[]{:S(2)}, u32[]{:S(2)}) collective-permute-start(bf16[576,2048]{1,0:T(8,128)(2,1)S(1)} %slice.345), channel_id=1, source_target_pairs={{4,0},{0,4},{5,1},{1,5},{6,2},{2,6},{7,3},{3,7},{12,8},{8,12},{13,... | collective-permute-start | bytes 7077896 | tf_op jit(solution)/shard_map/ppermute | solution.py:161
  499.6 4.6 collective-permute-start.14
  503.1 28.9 %collective-permute-start.21 = (bf16[288,2048]{1,0:T(8,128)(2,1)S(1)}, bf16[288,2048]{1,0:T(8,128)(2,1)S(1)}, u32[]{:S(2)}, u32[]{:S(2)}) collective-permute-start(bf16[288,2048]{1,0:T(8,128)(2,1)S(1)} %slice.349), channel_id=1, source_target_pairs={{1,0},{0,1},{3,2},{2,3},{5,4},{4,5},{7,6},{6,7},{9,8},{8,9},{11,10... | collective-permute-start | bytes 3538952 | tf_op jit(solution)/shard_map/ppermute | solution.py:166
  505.5 51.2 %collective-permute-start.15 = (bf16[288,2048]{1,0:T(8,128)(2,1)S(1)}, bf16[288,2048]{1,0:T(8,128)(2,1)S(1)}, u32[]{:S(2)}, u32[]{:S(2)}) collective-permute-start(bf16[288,2048]{1,0:T(8,128)(2,1)S(1)} %slice.350), channel_id=1, source_target_pairs={{1,0},{0,1},{3,2},{2,3},{5,4},{4,5},{7,6},{6,7},{9,8},{8,9},{11,10... | collective-permute-start | bytes 3538952 | tf_op jit(solution)/shard_map/ppermute | solution.py:166
  561.1 27.4 %collective-permute-start.22 = (bf16[288,2048]{1,0:T(8,128)(2,1)S(1)}, bf16[288,2048]{1,0:T(8,128)(2,1)S(1)}, u32[]{:S(2)}, u32[]{:S(2)}) collective-permute-start(bf16[288,2048]{1,0:T(8,128)(2,1)S(1)} %get-tuple-element.482), channel_id=1, source_target_pairs={{1,0},{0,1},{3,2},{2,3},{5,4},{4,5},{7,6},{6,7},{9,8},{8,9},{11,10... | collective-permute-start | bytes 3538952 | tf_op jit(solution)/shard_map/ppermute | solution.py:152
  591.2 13.2 %collective-permute-start.23 = (bf16[576,2048]{1,0:T(8,128)(2,1)}, bf16[576,2048]{1,0:T(8,128)(2,1)}, u32[]{:S(2)}, u32[]{:S(2)}) collective-permute-start(bf16[576,2048]{1,0:T(8,128)(2,1)} %pad_maximum_fusion.9), channel_id=1, source_target_pairs={{4,0},{0,4},{5,1},{1,5},{6,2},{2,6},{7,3},{3,7},{12,8},{8,12},{13,... | collective-permute-start | bytes 7077896 | tf_op jit(solution)/shard_map/ppermute | solution.py:154
  604.3 303.6 %reduce-scatter.4.cloned.1.call-start = ((), (), s32[]{:S(2)}) async-start(), calls=%async_computation.6 | async-start | bytes 7864320 | tf_op jit(solution)/shard_map/reduce_scatter | solution.py:184
  710.9 199.8 %reduce-scatter.6.cloned.1.call-start = ((), (), s32[]{:S(2)}) async-start(), calls=%async_computation.7 | async-start | bytes 15728640 | tf_op jit(solution)/shard_map/reduce_scatter | solution.py:184
  760.5 4.6 collective-permute-start.24
  760.8 9.6 collective-permute-start.16
  769.6 40.8 %collective-permute-start.25 = (bf16[288,2048]{1,0:T(8,128)(2,1)}, bf16[288,2048]{1,0:T(8,128)(2,1)S(1)}, u32[]{:S(2)}, u32[]{:S(2)}) collective-permute-start(bf16[288,2048]{1,0:T(8,128)(2,1)} %slice.348), channel_id=1, source_target_pairs={{1,0},{0,1},{3,2},{2,3},{5,4},{4,5},{7,6},{6,7},{9,8},{8,9},{11,10... | collective-permute-start | bytes 3538952 | tf_op jit(solution)/shard_map/ppermute | solution.py:166
  770.4 43.6 %copy-start.78 = (f32[2048]{0:T(1024)S(1)}, f32[2048]{0:T(1024)}, u32[]{:S(2)}) copy-start(f32[2048]{0:T(1024)} %get-tuple-element.424) | copy-start | bytes 24580
  770.4 43.6 %copy-start.88 = (f32[128]{0:T(128)S(1)}, f32[128]{0:T(128)}, u32[]{:S(2)}) copy-start(f32[128]{0:T(128)} %get-tuple-element.430) | copy-start | bytes 1540
  770.4 43.6 %copy-start.89 = (f32[128]{0:T(128)S(1)}, f32[128]{0:T(128)}, u32[]{:S(2)}) copy-start(f32[128]{0:T(128)} %get-tuple-element.428) | copy-start | bytes 1540
  770.4 116.9 %copy-start.83 = (f32[288]{0:T(512)S(1)}, f32[288]{0:T(512)}, u32[]{:S(2)}) copy-start(f32[288]{0:T(512)} %copy-done.82) | copy-start | bytes 3460
  893.0 19.9 %collective-permute-start.26 = (bf16[288,2048]{1,0:T(8,128)(2,1)}, bf16[288,2048]{1,0:T(8,128)(2,1)}, u32[]{:S(2)}, u32[]{:S(2)}) collective-permute-start(bf16[288,2048]{1,0:T(8,128)(2,1)} %get-tuple-element.478), channel_id=1, source_target_pairs={{0,0},{2,4},{4,2},{6,6},{1,1},{3,5},{5,3},{7,7},{8,8},{10,12},{12,... | collective-permute-start | bytes 3538952 | tf_op jit(solution)/shard_map/ppermute | solution.py:147
  907.9 8.1 collective-permute-start.31
  910.2 12.9 %collective-permute-start.27 = (bf16[256,1536]{0,1:T(8,128)(2,1)}, bf16[256,1536]{0,1:T(8,128)(2,1)}, u32[]{:S(2)}, u32[]{:S(2)}) collective-permute-start(bf16[256,1536]{0,1:T(8,128)(2,1)} %broadcast_select_fusion.15), channel_id=1, source_target_pairs={{4,0},{0,4},{5,1},{1,5},{6,2},{2,6},{7,3},{3,7},{12,8},{8,12},{13,... | collective-permute-start | bytes 2359304 | tf_op jit(solution)/shard_map/ppermute | solution.py:188
  912.8 12.6 %collective-permute-start.29 = (bf16[256,3072]{0,1:T(8,128)(2,1)S(1)}, bf16[256,3072]{0,1:T(8,128)(2,1)S(1)}, u32[]{:S(2)}, u32[]{:S(2)}) collective-permute-start(bf16[256,3072]{0,1:T(8,128)(2,1)S(1)} %broadcast_select_fusion.3), channel_id=1, source_target_pairs={{4,0},{0,4},{5,1},{1,5},{6,2},{2,6},{7,3},{3,7},{12,8},{8,12},{13,... | collective-permute-start | bytes 4718600 | tf_op jit(solution)/shard_map/ppermute | solution.py:188
  917.0 90.4 %collective-permute-start.32 = (bf16[256,1536]{0,1:T(8,128)(2,1)S(1)}, bf16[256,1536]{0,1:T(8,128)(2,1)S(1)}, u32[]{:S(2)}, u32[]{:S(2)}) collective-permute-start(bf16[256,1536]{0,1:T(8,128)(2,1)S(1)} %broadcast_select_fusion.7), channel_id=1, source_target_pairs={{2,0},{0,2},{3,1},{1,3},{6,4},{4,6},{7,5},{5,7},{10,8},{8,10},{11,... | collective-permute-start | bytes 2359304 | tf_op jit(solution)/shard_map/ppermute | solution.py:190
  925.4 82.0 %copy-start.40 = (bf16[256,1536]{0,1:T(8,128)(2,1)S(1)}, bf16[256,1536]{0,1:T(8,128)(2,1)}, u32[]{:S(2)}) copy-start(bf16[256,1536]{0,1:T(8,128)(2,1)} %copy-done.39) | copy-start | bytes 2359300
  925.4 98.9 %collective-permute-start.28 = (bf16[256,1536]{0,1:T(8,128)(2,1)}, bf16[256,1536]{0,1:T(8,128)(2,1)}, u32[]{:S(2)}, u32[]{:S(2)}) collective-permute-start(bf16[256,1536]{0,1:T(8,128)(2,1)} %broadcast_select_fusion.8), channel_id=1, source_target_pairs={{2,0},{0,2},{3,1},{1,3},{6,4},{4,6},{7,5},{5,7},{10,8},{8,10},{11,... | collective-permute-start | bytes 2359304 | tf_op jit(solution)/shard_map/ppermute | solution.py:190
  927.1 130.9 %collective-permute-start.30 = (bf16[256,3072]{0,1:T(8,128)(2,1)}, bf16[256,3072]{0,1:T(8,128)(2,1)}, u32[]{:S(2)}, u32[]{:S(2)}) collective-permute-start(bf16[256,3072]{0,1:T(8,128)(2,1)} %broadcast_select_fusion), channel_id=1, source_target_pairs={{2,0},{0,2},{3,1},{1,3},{6,4},{4,6},{7,5},{5,7},{10,8},{8,10},{11,... | collective-permute-start | bytes 4718600 | tf_op jit(solution)/shard_map/ppermute | solution.py:190
  (95 other events, 644.5 us)
Sparse Core Ops, SparseCore 0:
  54.3 71.2 all-gather.6
  179.3 123.1 all-gather.8
  333.9 68.6 all-gather.10
  604.4 68.4 reduce-scatter.7
  711.0 68.9 reduce-scatter.3
  783.0 123.3 reduce-scatter.5
